TPU v7x, 128 devices: a whole 4x4x4 slice. The times are simulated.
128 devices in a mesh: blk: 32 (over x, z, core), grp: 4 (over y).
Axes of the slice: x: 4, y: 4, z: 4, core: 2. Of those that a mesh axis runs over, the one named last changes fastest.
Arguments:
- statistics: float32 [4, 64, 512, 512], P('grp', 'blk'), as said below
- gradients: bfloat16 [4, 16, 512, 14336], P('grp', None, None, 'blk'), may hold values from -6 to 6
- live_counts: int32 [4, 32], P('grp'), may hold values from 0 to 2, as said below
- slot_row: int32 [4, 64], P('grp'), may hold values from 0 to 15, as said below
- sweeps: int32 [4, 64], P('grp', 'blk'), may hold values from 1 to 2, as said below
Outputs:
- updates: bfloat16 [4, 16, 512, 14336], P('grp', None, None, 'blk')
- off_max: float32 [2], replicated
Inputs may be any that keep to these rules, and one draw needn't show every extreme that they name: `live_counts`: the live slots of one index of grp number exactly 16; in every draw some device of each grp index has 2 live slots. `slot_row`: over the live slots of one index of grp each row block 0 to 15 appears exactly once. In each index of grp some live slot has 2 sweeps. `statistics`: every block is symmetric positive definite.
All inputs are finite; a program needn't handle non-finite values.
Results may differ from a plain program's by a relative error of at most 0.0051.
Values may be sent and summed in bfloat16 or wider, within the bound.
A program may use at most 192 MiB of HBM per device.

v0:
```python
import functools
import jax
import jax.numpy as jnp
from jax import lax
from jax.sharding import Mesh
from jax.sharding import PartitionSpec as P

MAXS = 2
BLK = ("blk_0", "blk_1", "blk_2")
BLK_GRP = ("blk_0", "blk_1", "blk_2", "grp")
damping = 0.01
pairings = ((0, 1, 2, 3), (0, 2, 1, 3), (0, 3, 1, 2))
highest = lax.Precision.HIGHEST


def by_axis(x, axes):
    return functools.reduce(lax.pmax, axes, x)


def regroup_cols(values, pairing, group_width):
    return jnp.concatenate(
        [values[:, member * group_width : (member + 1) * group_width] for member in pairing], axis=1
    )


def regroup(values, pairing, group_width):
    stacked = jnp.concatenate(
        [values[member * group_width : (member + 1) * group_width] for member in pairing], axis=0
    )
    return regroup_cols(stacked, pairing, group_width)


def angle_block(square_sub):
    group_width = square_sub.shape[-1] // 2
    diagonal = jnp.diagonal(square_sub, axis1=1, axis2=2)
    lower_diag = diagonal[:, :group_width, None]
    upper_diag = diagonal[:, None, group_width:]
    coupling = square_sub[:, :group_width, group_width:]
    difference = upper_diag - lower_diag
    bottom = (
        difference * difference
        + 4.0 * coupling * coupling
        + damping * (lower_diag + upper_diag) ** 2
    )
    return coupling * difference / bottom


def rotation_of(square_sub):
    angles = angle_block(square_sub)
    group_width = angles.shape[-1]
    identity = jnp.eye(group_width, dtype=jnp.float32)
    outer = jnp.einsum("hpq,hrq->hpr", angles, angles, precision=highest)
    inner = jnp.einsum("hqp,hqr->hpr", angles, angles, precision=highest)
    left_factor = jnp.linalg.cholesky(identity + 0.25 * outer)
    right_factor = jnp.linalg.cholesky(identity + 0.25 * inner)
    top_rows = jnp.concatenate([identity - 0.25 * outer, angles], axis=2)
    low_rows = jnp.concatenate([-jnp.swapaxes(angles, 1, 2), identity - 0.25 * inner], axis=2)
    top_half = jax.scipy.linalg.cho_solve((left_factor, True), top_rows)
    low_half = jax.scipy.linalg.cho_solve((right_factor, True), low_rows)
    return jnp.concatenate([top_half, low_half], axis=1)


def rotate_round(matrix, vectors, pairing):
    block_size = matrix.shape[0]
    group_width = block_size // 4
    restore = [pairing.index(member) for member in range(4)]
    matrix = regroup(matrix, pairing, group_width)
    vectors = regroup_cols(vectors, pairing, group_width)
    half_size = 2 * group_width
    square_sub = jnp.stack([matrix[:half_size, :half_size], matrix[half_size:, half_size:]])
    rotation = rotation_of(square_sub)
    row_part = jnp.einsum(
        "hpq,hpc->hqc", rotation, matrix.reshape(2, half_size, block_size), precision=highest
    )
    row_part = row_part.reshape(block_size, block_size)
    matrix = jnp.einsum(
        "rhp,hpq->rhq", row_part.reshape(block_size, 2, half_size), rotation, precision=highest
    )
    matrix = matrix.reshape(block_size, block_size)
    vectors = jnp.einsum(
        "rhp,hpq->rhq", vectors.reshape(block_size, 2, half_size), rotation, precision=highest
    )
    vectors = vectors.reshape(block_size, block_size)
    return (regroup(matrix, restore, group_width), regroup_cols(vectors, restore, group_width))


def one_sweep(matrix, vectors):
    for pairing in pairings:
        matrix, vectors = rotate_round(matrix, vectors, pairing)
    return (matrix, vectors)


def keep_both(matrix, vectors):
    return (matrix, vectors)


def off_norm(matrix):
    block_size = matrix.shape[0]
    on_diagonal = lax.broadcasted_iota(
        jnp.int32, (block_size, block_size), 0
    ) == lax.broadcasted_iota(jnp.int32, (block_size, block_size), 1)
    outside = jnp.where(on_diagonal, 0.0, matrix)
    return jnp.sqrt(jnp.sum(outside * outside) / jnp.sum(matrix * matrix))


def root_factor(matrix, vectors):
    scales = jnp.power(jnp.diagonal(matrix), -0.25)
    return jnp.dot(vectors * scales[None, :], vectors.T, precision=highest).astype(jnp.bfloat16)


def per_device(statistics, gradients, live_counts, slot_row, sweeps):
    matrices = statistics[0]
    slot_count = matrices.shape[0]
    block_size = matrices.shape[1]
    row_count = gradients.shape[1]
    blk_rank = lax.axis_index(BLK)
    own_live = lax.dynamic_index_in_dim(live_counts[0], blk_rank, 0, keepdims=False)
    own_sweeps = sweeps[0]
    identity = jnp.eye(block_size, dtype=jnp.float32)
    states = [matrices[slot_index] for slot_index in range(slot_count)]
    eigen_bases = [identity for slot_index in range(slot_count)]
    live_flags = [slot_index < own_live for slot_index in range(slot_count)]
    sweep_list = [own_sweeps[slot_index] for slot_index in range(slot_count)]
    local_peaks = jnp.zeros((MAXS,), jnp.float32)
    for slot_index in range(slot_count):
        for sweep_index in range(MAXS):
            active = jnp.logical_and(live_flags[slot_index], sweep_list[slot_index] > sweep_index)
            states[slot_index], eigen_bases[slot_index] = lax.cond(
                active, one_sweep, keep_both, states[slot_index], eigen_bases[slot_index]
            )
            local_peaks = local_peaks.at[sweep_index].max(
                jnp.where(active, off_norm(states[slot_index]), jnp.float32(0.0))
            )
    off_max = by_axis(local_peaks, BLK_GRP)
    blank_factor = jnp.zeros((block_size, block_size), jnp.bfloat16)
    factor_list = [
        jnp.where(
            live_flags[slot_index],
            root_factor(states[slot_index], eigen_bases[slot_index]),
            blank_factor,
        )
        for slot_index in range(slot_count)
    ]
    factors = jnp.stack(factor_list)
    row_ids = lax.iota(jnp.int32, row_count)
    gathered = lax.all_gather(factors, BLK, axis=0, tiled=True)
    slot_total = gathered.shape[0]
    slot_ids = lax.iota(jnp.int32, slot_total)
    is_live = slot_ids % slot_count < jnp.repeat(live_counts[0], slot_count)
    matches = (slot_row[0][None, :] == row_ids[:, None]) & is_live[None, :]
    slot_of = jnp.sum(jnp.where(matches, slot_ids[None, :], 0), axis=1)
    chosen = jnp.take(gathered, slot_of, axis=0)
    updates = jnp.einsum("kij,kjc->kic", chosen, gradients[0], preferred_element_type=jnp.float32)
    return (updates.astype(jnp.bfloat16)[None], off_max)


def solution(mesh):
    split = Mesh(
        mesh.devices.reshape(4, 4, 2, mesh.shape["grp"]), ("blk_0", "blk_1", "blk_2", "grp")
    )
    return jax.shard_map(
        per_device,
        mesh=split,
        in_specs=(
            P("grp", BLK, None, None),
            P("grp", None, None, BLK),
            P("grp", None),
            P("grp", None),
            P("grp", BLK),
        ),
        out_specs=(P("grp", None, None, BLK), P()),
        check_vma=False,
    )
```

profile of v0, /device:TPU:1, one launch (start us, length us, event | category | flops | bytes accessed | tf_op | source)
XLA Modules:
  0.0 1782.7 jit_solution(11419021902682509797)
XLA Ops:
  14.5 2.7 slice_bitcast_fusion.9
  17.2 372.8 %conditional.4 = (f32[512,512]{0,1:T(8,128)S(1)}, f32[512,512]{0,1:T(8,128)S(1)}) conditional(s32[]{:T(128)} %convert_element_type.155, (f32[512,512]{1,0:T(8,128)S(1)}, f32[512,512]{0,1:T(8,128)S(1)}) %tuple.70, (f32[512,512]{1,0:T(8,128)S(1)}, f32[512,512]{0,1:T(8,128)S(1)}) %tuple.70), branch_computations={%region_1.2_spmd, %region_2.7_spmd} | conditional | flops 8781105152 | bytes 108000352 | solution.py:128
  18.2 17.2 copy.767
  38.6 23.5 %custom-call.84 = f32[2,128,128]{2,1,0:T(8,128)S(1)} custom-call(f32[2,128,128]{2,1,0:T(8,128)S(1)} %fusion.75), custom_call_target="Cholesky" | custom-call | tf_op jit(solution)/shard_map/cond/branch_1_fun/jit(cholesky)/cholesky | solution.py:55
  62.6 23.5 %custom-call.82 = f32[2,128,128]{2,1,0:T(8,128)S(1)} custom-call(f32[2,128,128]{2,1,0:T(8,128)S(1)} %copy.773), custom_call_target="Cholesky" | custom-call | tf_op jit(solution)/shard_map/cond/branch_1_fun/jit(cholesky)/cholesky | solution.py:54
  87.0 20.1 %custom-call.83 = f32[2,1,128,128]{2,3,1,0:T(8,128)S(1)} custom-call(f32[2,1,128,128]{3,2,1,0:T(8,128)S(1)} %get-tuple-element.295), custom_call_target="InvertDiagBlocksLowerTriangular" | custom-call | tf_op jit(solution)/shard_map/cond/branch_1_fun/jit(_cho_solve)/vmap()/triangular_solve | solution.py:58
  108.0 20.5 %custom-call.85 = f32[2,1,128,128]{2,3,1,0:T(8,128)S(1)} custom-call(f32[2,1,128,128]{3,2,1,0:T(8,128)} %get-tuple-element.296), custom_call_target="InvertDiagBlocksLowerTriangular" | custom-call | tf_op jit(solution)/shard_map/cond/branch_1_fun/jit(_cho_solve)/vmap()/triangular_solve | solution.py:59
  142.2 16.6 copy.788
  163.4 23.5 %custom-call.86 = f32[2,128,128]{2,1,0:T(8,128)S(1)} custom-call(f32[2,128,128]{2,1,0:T(8,128)S(1)} %fusion.71), custom_call_target="Cholesky" | custom-call | tf_op jit(solution)/shard_map/cond/branch_1_fun/jit(cholesky)/cholesky | solution.py:54
  187.0 23.5 %custom-call.88 = f32[2,128,128]{2,1,0:T(8,128)S(1)} custom-call(f32[2,128,128]{2,1,0:T(8,128)S(1)} %fusion.67), custom_call_target="Cholesky" | custom-call | tf_op jit(solution)/shard_map/cond/branch_1_fun/jit(cholesky)/cholesky | solution.py:55
  210.9 19.9 %custom-call.87 = f32[2,1,128,128]{2,3,1,0:T(8,128)S(1)} custom-call(f32[2,1,128,128]{3,2,1,0:T(8,128)S(1)} %get-tuple-element.293), custom_call_target="InvertDiagBlocksLowerTriangular" | custom-call | tf_op jit(solution)/shard_map/cond/branch_1_fun/jit(_cho_solve)/vmap()/triangular_solve | solution.py:58
  231.6 19.7 %custom-call.89 = f32[2,1,128,128]{2,3,1,0:T(8,128)S(1)} custom-call(f32[2,1,128,128]{3,2,1,0:T(8,128)S(1)} %get-tuple-element.294), custom_call_target="InvertDiagBlocksLowerTriangular" | custom-call | tf_op jit(solution)/shard_map/cond/branch_1_fun/jit(_cho_solve)/vmap()/triangular_solve | solution.py:59
  255.1 3.4 fusion.14
  267.4 16.5 copy.812
  287.0 23.9 %custom-call.92 = f32[2,128,128]{2,1,0:T(8,128)S(1)} custom-call(f32[2,128,128]{2,1,0:T(8,128)S(1)} %fusion.59), custom_call_target="Cholesky" | custom-call | tf_op jit(solution)/shard_map/cond/branch_1_fun/jit(cholesky)/cholesky | solution.py:55
  311.5 23.5 %custom-call.90 = f32[2,128,128]{2,1,0:T(8,128)S(1)} custom-call(f32[2,128,128]{2,1,0:T(8,128)S(1)} %copy.818), custom_call_target="Cholesky" | custom-call | tf_op jit(solution)/shard_map/cond/branch_1_fun/jit(cholesky)/cholesky | solution.py:54
  336.8 19.7 %custom-call.91 = f32[2,1,128,128]{2,3,1,0:T(8,128)S(1)} custom-call(f32[2,1,128,128]{3,2,1,0:T(8,128)S(1)} %get-tuple-element.291), custom_call_target="InvertDiagBlocksLowerTriangular" | custom-call | tf_op jit(solution)/shard_map/cond/branch_1_fun/jit(_cho_solve)/vmap()/triangular_solve | solution.py:58
  357.3 19.8 %custom-call.93 = f32[2,1,128,128]{2,3,1,0:T(8,128)S(1)} custom-call(f32[2,1,128,128]{3,2,1,0:T(8,128)S(1)} %get-tuple-element.292), custom_call_target="InvertDiagBlocksLowerTriangular" | custom-call | tf_op jit(solution)/shard_map/cond/branch_1_fun/jit(_cho_solve)/vmap()/triangular_solve | solution.py:59
  380.1 3.4 fusion.12
  392.6 15.4 conditional.5
  408.0 8.9 gather_fusion.12
  416.9 10.5 conditional.6
  431.3 11.1 conditional.7
  442.4 8.5 gather_fusion.13
  452.9 2.6 fusion.410
  470.0 811.0 %pmax.28 = f32[2]{0:T(128)S(1)} all-reduce(f32[2]{0:T(128)S(1)} %maximum_dynamic-update-slice_fusion), channel_id=1, replica_groups=mesh['blk_0'=4,'blk_1'=4,'blk_2'=2,'grp'=4] {'blk_0'}, use_global_device_ids=true, to_apply=%region_19.22 | all-reduce | flops 2 | bytes 16 | tf_op jit(solution)/shard_map/pmax | solution.py:17
  1281.0 6.0 pmax.29
  1286.9 9.1 pmax.30
  1296.0 390.1 %pmax.31 = f32[2]{0:T(128)} all-reduce(f32[2]{0:T(128)S(1)} %pmax.30), channel_id=1, replica_groups=mesh['blk_0'=4,'blk_1'=4,'blk_2'=2,'grp'=4] {'grp'}, use_global_device_ids=true, to_apply=%region_22.25 | all-reduce | flops 2 | bytes 16 | tf_op jit(solution)/shard_map/pmax | solution.py:17
  1687.2 71.6 %all-gather.2.cloned.1.call-done = bf16[64,512,512]{2,1,0:T(8,128)(2,1)} async-done(((bf16[2,512,512]{2,1,0:T(8,128)(2,1)}), bf16[64,512,512]{2,1,0:T(8,128)(2,1)}) %all-gather.2.cloned.1.call-update) | async-done | bytes 33554448 | tf_op jit(solution)/shard_map/all_gather | solution.py:146
  1758.8 6.3 gather_fusion.14
  1765.0 10.6 convert_bitcast_fusion
  (153 shorter events, 80.9 us)
Async XLA Ops:
  7.2 1751.6 %all-gather.2.cloned.1.call-start = ((), (), s32[]{:S(2)}) async-start(), calls=%async_computation | async-start | bytes 34603008 | tf_op jit(solution)/shard_map/all_gather | solution.py:146
  17.2 193.3 %copy-start.17 = (pred[128,128]{1,0:T(8,128)(4,1)}, pred[128,128]{1,0:T(8,128)(4,1)S(1)}, u32[]{:S(2)}) copy-start(pred[128,128]{1,0:T(8,128)(4,1)S(1)} %iota_compare_fusion.7) | copy-start | bytes 49156 | tf_op jit(solution)/shard_map/cond
  17.2 193.5 %copy-start.13 = (pred[128,128]{1,0:T(8,128)(4,1)}, pred[128,128]{1,0:T(8,128)(4,1)S(1)}, u32[]{:S(2)}) copy-start(pred[128,128]{1,0:T(8,128)(4,1)S(1)} %iota_compare_fusion.6) | copy-start | bytes 49156 | tf_op jit(solution)/shard_map/cond
  431.3 1254.9 %copy-start.21 = (s32[1,32]{1,0:T(1,128)S(1)}, s32[1,32]{1,0:T(1,128)}, u32[]{:S(2)}) copy-start(s32[1,32]{1,0:T(1,128)} %param.26) | copy-start | bytes 388
Sparse Core Ops, SparseCore 0:
  456.7 1302.0 all-gather.1
where the time goes:
time: 1800 us; the launch traced here: 1780 us
  blocking collectives  1220 us (68%)
  other arithmetic  282 us (16%)
  local copies, waits for them, and re-layouts  112 us (6%)
  waiting for transfers between devices  71.6 us (4%)
  matrix products  44.1 us (2%)
  loops' own time  32.1 us (2%)
  between operations  24.6 us (1%)
    pmax x4, blocking collectives, by_axis(): return functools.reduce(lax.pmax, axes, x)  1220 us
    all_gather x1, waiting for transfers between devices, per_device(): gathered = lax.all_gather(factors, BLK, axis=0, tiled=True)  71.6 us
    another operation x9, other arithmetic, rotation_of(): left_factor = jnp.linalg.cholesky(identity + 0.25 * outer)  71.5 us
    another operation x6, other arithmetic, rotation_of(): right_factor = jnp.linalg.cholesky(identity + 0.25 * inner)  71.2 us
    another operation x7, other arithmetic, rotation_of(): top_half = jax.scipy.linalg.cho_solve((left_factor, True), top_rows)  61.4 us
    another operation x3, other arithmetic, rotation_of(): low_half = jax.scipy.linalg.cho_solve((right_factor, True), low_rows)  60 us
    another operation x4, local copies, waits for them, and re-layouts, rotate_round(): jnp.stack([matrix[:half_size, :half_size], matrix[half_size:, half_size:]])  50.3 us
  transfers between devices with their start and end apart: 1, of which 1 were waited for; matrix products, arithmetic and copies ran while one was open for 0% of the time, Pallas kernels for 0%

commit v1 on v0

--- a/solution.py
+++ b/solution.py
@@ -143,7 +143,8 @@
     ]
     factors = jnp.stack(factor_list)
     row_ids = lax.iota(jnp.int32, row_count)
-    gathered = lax.all_gather(factors, BLK, axis=0, tiled=True)
+    sent = jnp.stack([factors] * lax.axis_size(BLK))
+    gathered = jnp.concatenate(lax.all_to_all(sent, BLK, 0, 0), axis=0)
     slot_total = gathered.shape[0]
     slot_ids = lax.iota(jnp.int32, slot_total)
     is_live = slot_ids % slot_count < jnp.repeat(live_counts[0], slot_count)

time: 1800 us -> 2320 us (1.29)
  starting transfers between devices: 0.04 us -> 840 us
  blocking collectives: 1220 us -> 950 us
  waiting for transfers between devices: 71.6 us -> 0.01 us
    all_to_all x0 -> x1, starting transfers between devices: none -> 840 us  [per_device(): gathered = jnp.concatenate(lax.all_to_all(sent, BLK, 0, 0), axis=0)]
    pmax x4, blocking collectives: 1220 us -> 950 us  [by_axis(): return functools.reduce(lax.pmax, axes, x)]
    all_gather x1 -> x0, waiting for transfers between devices: 71.6 us -> none  [per_device(): gathered = lax.all_gather(factors, BLK, axis=0, tiled=True)]
  transfers between devices with their start and end apart: 1 -> 1, of which waited for: 1 -> 0; matrix products, arithmetic and copies ran while one was open for 0% -> 0% of each run, Pallas kernels for 0% -> 0%
where the time goes in v1:
time: 2320 us; the launch traced here: 2300 us
  blocking collectives  950 us (41%)
  starting transfers between devices  840 us (36%)
  other arithmetic  289 us (12%)
  local copies, waits for them, and re-layouts  133 us (6%)
  matrix products  46.1 us (2%)
  loops' own time  29.1 us (1%)
    pmax x4, blocking collectives, by_axis(): return functools.reduce(lax.pmax, axes, x)  950 us
    all_to_all x1, starting transfers between devices, per_device(): gathered = jnp.concatenate(lax.all_to_all(sent, BLK, 0, 0), axis=0)  840 us
    another operation x9, other arithmetic, rotation_of(): left_factor = jnp.linalg.cholesky(identity + 0.25 * outer)  73.2 us
    another operation x6, other arithmetic, rotation_of(): right_factor = jnp.linalg.cholesky(identity + 0.25 * inner)  72.6 us
    another operation x7, other arithmetic, rotation_of(): top_half = jax.scipy.linalg.cho_solve((left_factor, True), top_rows)  63.2 us
    another operation x3, other arithmetic, rotation_of(): low_half = jax.scipy.linalg.cho_solve((right_factor, True), low_rows)  60 us
    another operation x4, local copies, waits for them, and re-layouts, rotate_round(): jnp.stack([matrix[:half_size, :half_size], matrix[half_size:, half_size:]])  51.7 us
  transfers between devices with their start and end apart: 1, of which 0 were waited for; matrix products, arithmetic and copies ran while one was open for 0% of the time, Pallas kernels for 0%

profile of v1, /device:TPU:1, one launch (start us, length us, event | category | flops | bytes accessed | tf_op | source)
XLA Modules:
  0.0 2297.1 jit_solution(4518397182891227333)
XLA Ops:
  9.8 393.3 %conditional.4 = (f32[512,512]{0,1:T(8,128)S(1)}, f32[512,512]{0,1:T(8,128)S(1)}) conditional(s32[]{:T(128)} %convert_element_type.155, (f32[512,512]{1,0:T(8,128)S(1)}, f32[512,512]{0,1:T(8,128)S(1)}) %tuple.70, (f32[512,512]{1,0:T(8,128)S(1)}, f32[512,512]{0,1:T(8,128)S(1)}) %tuple.70), branch_computations={%region_1.2_spmd, %region_2.7_spmd} | conditional | flops 8781105152 | bytes 119010536 | solution.py:128
  10.7 17.2 copy.487
  31.1 23.5 %custom-call.84 = f32[2,128,128]{2,1,0:T(8,128)S(1)} custom-call(f32[2,128,128]{2,1,0:T(8,128)S(1)} %fusion.75), custom_call_target="Cholesky" | custom-call | tf_op jit(solution)/shard_map/cond/branch_1_fun/jit(cholesky)/cholesky | solution.py:55
  55.2 23.5 %custom-call.82 = f32[2,128,128]{2,1,0:T(8,128)S(1)} custom-call(f32[2,128,128]{2,1,0:T(8,128)S(1)} %copy.493), custom_call_target="Cholesky" | custom-call | tf_op jit(solution)/shard_map/cond/branch_1_fun/jit(cholesky)/cholesky | solution.py:54
  79.0 20.1 custom-call.83
  100.0 19.7 custom-call.85
  127.8 3.1 convolution_bitcast_fusion.2
  133.3 17.3 copy.508
  164.2 24.9 %custom-call.88 = f32[2,128,128]{2,1,0:T(8,128)} custom-call(f32[2,128,128]{2,1,0:T(8,128)} %fusion.67), custom_call_target="Cholesky" | custom-call | tf_op jit(solution)/shard_map/cond/branch_1_fun/jit(cholesky)/cholesky | solution.py:55
  189.8 24.3 %custom-call.86 = f32[2,128,128]{2,1,0:T(8,128)S(1)} custom-call(f32[2,128,128]{2,1,0:T(8,128)} %fusion.71), custom_call_target="Cholesky" | custom-call | tf_op jit(solution)/shard_map/cond/branch_1_fun/jit(cholesky)/cholesky | solution.py:54
  217.0 20.7 custom-call.87
  239.4 20.5 custom-call.89
  271.6 3.1 convolution_bitcast_fusion.1
  278.2 17.2 copy.532
  299.2 23.9 %custom-call.92 = f32[2,128,128]{2,1,0:T(8,128)S(1)} custom-call(f32[2,128,128]{2,1,0:T(8,128)S(1)} %fusion.59), custom_call_target="Cholesky" | custom-call | tf_op jit(solution)/shard_map/cond/branch_1_fun/jit(cholesky)/cholesky | solution.py:55
  323.7 23.5 %custom-call.90 = f32[2,128,128]{2,1,0:T(8,128)S(1)} custom-call(f32[2,128,128]{2,1,0:T(8,128)S(1)} %copy.538), custom_call_target="Cholesky" | custom-call | tf_op jit(solution)/shard_map/cond/branch_1_fun/jit(cholesky)/cholesky | solution.py:54
  349.0 19.7 custom-call.91
  369.5 19.8 custom-call.93
  399.5 3.1 convolution_bitcast_fusion
  406.4 12.9 conditional.6
  423.8 11.8 conditional.5
  435.6 8.7 gather_fusion.12
  444.4 9.3 conditional.7
  453.7 9.0 gather_fusion.13
  467.4 11.0 stack.155
  478.4 839.9 %all-to-all-start = ((bf16[32,2,512,512]{3,2,1,0:T(8,128)(2,1)}), bf16[32,2,512,512]{3,2,1,0:T(8,128)(2,1)}, u32[]{:S(2)}, u32[]{:S(2)}) async-start(bf16[32,2,512,512]{3,2,1,0:T(8,128)(2,1)} %stack.155), calls=%async_computation | async-start | bytes 67108864 | tf_op jit(solution)/shard_map/all_to_all | solution.py:147
  1330.2 479.8 %pmax.28 = f32[2]{0:T(128)S(1)} all-reduce(f32[2]{0:T(128)S(1)} %maximum_dynamic-update-slice_fusion), channel_id=1, replica_groups=mesh['blk_0'=4,'blk_1'=4,'blk_2'=2,'grp'=4] {'blk_0'}, use_global_device_ids=true, to_apply=%region_19.22 | all-reduce | flops 2 | bytes 16 | tf_op jit(solution)/shard_map/pmax | solution.py:17
  1810.0 62.5 %pmax.29 = f32[2]{0:T(128)S(1)} all-reduce(f32[2]{0:T(128)S(1)} %pmax.28), channel_id=1, replica_groups=mesh['blk_0'=4,'blk_1'=4,'blk_2'=2,'grp'=4] {'blk_1'}, use_global_device_ids=true, to_apply=%region_20.23 | all-reduce | flops 2 | bytes 16 | tf_op jit(solution)/shard_map/pmax | solution.py:17
  1872.4 5.1 pmax.30
  1877.6 402.1 %pmax.31 = f32[2]{0:T(128)} all-reduce(f32[2]{0:T(128)S(1)} %pmax.30), channel_id=1, replica_groups=mesh['blk_0'=4,'blk_1'=4,'blk_2'=2,'grp'=4] {'grp'}, use_global_device_ids=true, to_apply=%region_22.25 | all-reduce | flops 2 | bytes 16 | tf_op jit(solution)/shard_map/pmax | solution.py:17
  2280.0 6.3 gather_fusion.14
  2286.3 10.6 convert_bitcast_fusion
  (169 shorter events, 97.1 us)
Async XLA Ops:
  78.7 20.5 copy-start.37
  78.9 20.3 copy-start.42
  124.8 139.4 %copy-start.8 = (f32[512,512]{0,1:T(8,128)S(1)}, f32[512,512]{0,1:T(8,128)}, u32[]{:S(2)}) copy-start(f32[512,512]{0,1:T(8,128)} %pad_maximum_fusion.7) | copy-start | bytes 3145732 | tf_op jit(solution)/shard_map/cond
  131.7 0.7 copy-start.23
  259.9 1.7 copy-start.32
  275.6 1.0 copy-start.12
  276.7 0.7 copy-start.22
  423.8 11.9 copy-start
  478.4 845.6 %copy-start.1 = (f32[512,512]{0,1:T(8,128)S(1)}, f32[512,512]{0,1:T(8,128)}, u32[]{:S(2)}) copy-start(f32[512,512]{0,1:T(8,128)} %get-tuple-element.164) | copy-start | bytes 3145732
  478.4 1801.2 %copy-start.47 = (s32[1,32]{1,0:T(1,128)S(1)}, s32[1,32]{1,0:T(1,128)}, u32[]{:S(2)}) copy-start(s32[1,32]{1,0:T(1,128)} %param.26) | copy-start | bytes 388
  478.4 1801.4 %copy-start.48 = (s32[1,64]{1,0:T(1,128)S(1)}, s32[1,64]{1,0:T(1,128)}, u32[]{:S(2)}) copy-start(s32[1,64]{1,0:T(1,128)} %param.27) | copy-start | bytes 772
  478.4 1801.6 %all-to-all-start = ((bf16[32,2,512,512]{3,2,1,0:T(8,128)(2,1)}), bf16[32,2,512,512]{3,2,1,0:T(8,128)(2,1)}, u32[]{:S(2)}, u32[]{:S(2)}) async-start(bf16[32,2,512,512]{3,2,1,0:T(8,128)(2,1)} %stack.155), calls=%async_computation | async-start | bytes 67108864 | tf_op jit(solution)/shard_map/all_to_all | solution.py:147
